TPU v7x, 32 devices: a whole 2x2x4 slice. The times are simulated.
32 devices in a mesh: sta: 16 (over z, x, core), tpl: 2 (over y).
Axes of the slice: x: 2, y: 2, z: 4, core: 2. Of those that a mesh axis runs over, the one named last changes fastest.
Arguments:
- waveform: bfloat16 [16, 3, 4279], P('sta'), may hold values from -150 to 150
- templates: bfloat16 [128, 16, 1536], P('tpl', 'sta'), may hold values from -6 to 6
- lags: int32 [128, 16], P('tpl', 'sta'), may hold values from 0 to 3000
- present: int32 [128, 16], P('tpl', 'sta'), may hold values 0 or 1
Outputs:
- score: float32 [768, 128], P('sta', 'tpl')
- scale_mad: float32 [128], P('tpl')
- peak: float32 [768], P('sta')
All inputs are finite; a program needn't handle non-finite values. No bound on the sum of `present` on one device may be relied on, other than what follows from the above.
Results may differ from a plain program's by a relative error of at most 0.0003.
Values may be sent and summed in bfloat16 or wider, within the bound.
A program may use at most 64 MiB of HBM per device.

v0:
```python
import functools

import jax
import jax.numpy as jnp
from jax import lax
from jax.experimental import pallas as pl
from jax.experimental.pallas import tpu as pltpu
from jax.sharding import PartitionSpec as P

LEN = 512
LAG = 3000
BINS = 1024
TOUT_DEV = 48
LANES = 128
MESH = pl.DeviceIdType.MESH


def ceil_to(value, step):
    return -(-value // step) * step


def build_hankel(wave_ref, record, hankel):
    chans, samples = wave_ref.shape
    padded = record.shape[1]
    span = hankel.shape[2]
    record[...] = jnp.zeros_like(record)
    record[:, :samples] = wave_ref[...].astype(jnp.float32)
    piece = span
    for c in range(chans):
        for start in range(0, span, piece):
            size = min(piece, span - start)
            wide = size + LANES
            row = lax.broadcasted_iota(jnp.int32, (8, wide), 0)
            base = jnp.broadcast_to(record[c : c + 1, start : start + wide], (8, wide))
            for bit in (1, 2, 4):
                base = jnp.where((row & bit) != 0, pltpu.roll(base, wide - bit, 1), base)
            for g in range(LANES // 16):
                low = pltpu.roll(base, wide - 16 * g, 1) if g else base
                high = pltpu.roll(base, wide - 16 * g - 8, 1)
                both = jnp.concatenate([low[:, :size], high[:, :size]], axis=0)
                hankel[c, 16 * g : 16 * g + 16, start : start + size] = both.astype(jnp.bfloat16)


def correlate_blocks(blocks, stride, pattern_ref, hankel, corr):
    chans = hankel.shape[0]
    rows = pattern_ref.shape[0]
    pattern = pattern_ref[...]
    wide = pattern.astype(jnp.float32)
    factor = 1.0 / jnp.sqrt(jnp.sum(wide * wide, axis=1, keepdims=True) + 1e-06)
    for b in range(blocks):
        parts = []
        for c in range(chans):
            for q in range(LEN // LANES):
                begin = 2 * LANES * b + LANES * q
                parts.append(hankel[c, :, begin : begin + 2 * LANES])
        columns = jnp.concatenate(parts, axis=0)
        result = jnp.dot(pattern, columns, preferred_element_type=jnp.float32) * factor
        corr[pl.ds(2 * b, rows, stride=stride), :] = result[:, :LANES]
        corr[pl.ds(2 * b + 1, rows, stride=stride), :] = result[:, LANES:]


def deviation_scale(stack, groups, total):
    width = 512.0 / BINS
    count = stack.shape[0] // groups
    position = jnp.clip(jnp.abs(stack) / width - 0.5, 0.0, BINS - 1.0)
    lower = jnp.minimum(jnp.floor(position), BINS - 2.0)
    coarse = jnp.floor(lower * 0.125)
    fine = position - 8.0 * coarse
    sub = lax.broadcasted_iota(jnp.int32, (LANES, LANES), 0).astype(jnp.float32)
    few = lax.broadcasted_iota(jnp.int32, (16, LANES), 0).astype(jnp.float32)
    tables = []
    for t in range(groups):
        hots, weights = [], []
        for a in range(count):
            r = t * count + a
            hots.append((coarse[r : r + 1, :] == sub).astype(jnp.float32).astype(jnp.bfloat16))
            hat = jnp.maximum(1.0 - jnp.abs(fine[r : r + 1, :] - few), 0.0)
            first = hat.astype(jnp.bfloat16)
            left = hat - first.astype(jnp.float32)
            second = left.astype(jnp.bfloat16)
            third = (left - second.astype(jnp.float32)).astype(jnp.bfloat16)
            weights.append(jnp.concatenate([first, second, third], axis=0))
        hot = jnp.concatenate(hots, axis=1)
        weight = jnp.concatenate(weights, axis=1)
        found = lax.dot_general(weight, hot, (((1,), (1,)), ((), ())), preferred_element_type=jnp.float32)
        found = found[:16] + found[16:32] + found[32:48]
        tables.append(found[:8] + pltpu.roll(found[8:], 1, 1))
    counts = jnp.concatenate(tables, axis=0)
    row = lax.broadcasted_iota(jnp.int32, counts.shape, 0) & 7
    running = counts
    for step in (1, 2, 4):
        running = running + jnp.where(row >= step, pltpu.roll(running, step, 0), 0.0)
    sums = [jnp.broadcast_to(jnp.sum(t, axis=0, keepdims=True), (8, LANES)) for t in tables]
    sums = jnp.concatenate(sums, axis=0)
    upper = (
        lax.broadcasted_iota(jnp.int32, (LANES, LANES), 0) < lax.broadcasted_iota(jnp.int32, (LANES, LANES), 1)
    ).astype(jnp.float32)
    prior = jnp.dot(sums, upper, precision=lax.Precision.HIGHEST, preferred_element_type=jnp.float32)
    earlier = prior + (running - counts)
    share = jnp.clip((0.5 * total - earlier) / jnp.maximum(counts, 1.0), 0.0, 1.0)
    scales = []
    for t in range(groups):
        part = jnp.sum(share[8 * t : 8 * t + 8], axis=0, keepdims=True)
        scales.append(1.4826 * (width * jnp.sum(part, axis=1, keepdims=True)))
    return scales


def stack_kernel(n, m, own, blocks, stride, lags_hbm, present_hbm, wave_hbm, pattern_hbm, out_ref, lags_ref, present_ref, wave_ref, pattern_ref, load_sem, record, hankel, corr, moved, recv1, scored, send2, recv2, send3, recv3, send1_sem, recv1_sem, send2_sem, recv2_sem, send3_sem, recv3_sem):
    me, group = lax.axis_index("sta"), lax.axis_index("tpl")
    groups = send2.shape[1]
    chunk = moved.shape[1]
    count = chunk // groups
    rows = n * groups

    def peer(d):
        return lax.rem(me + d, n)

    def fellow(e):
        return lax.rem(group + e, m)

    loads = [
        pltpu.make_async_copy(source, target, load_sem.at[k])
        for k, (source, target) in enumerate(
            ((wave_hbm, wave_ref), (pattern_hbm, pattern_ref), (lags_hbm, lags_ref), (present_hbm, present_ref))
        )
    ]
    for load in loads:
        load.start()

    barrier = pltpu.get_barrier_semaphore()
    for e in range(m):

        def greet(d, carry):
            pl.semaphore_signal(barrier, inc=1, device_id={"sta": peer(d), "tpl": fellow(e)}, device_id_type=MESH)
            return carry

        lax.fori_loop(0 if e else 1, n, greet, 0)

    def copy1(d):
        return pltpu.make_async_remote_copy(
            src_ref=moved.at[d],
            dst_ref=recv1.at[d],
            send_sem=send1_sem.at[d],
            recv_sem=recv1_sem.at[d],
            device_id={"sta": peer(d), "tpl": group},
            device_id_type=MESH,
        )

    def copy2(d):
        return pltpu.make_async_remote_copy(
            src_ref=send2.at[peer(d)],
            dst_ref=recv2.at[me],
            send_sem=send2_sem.at[d],
            recv_sem=recv2_sem.at[d],
            device_id={"sta": peer(d), "tpl": group},
            device_id_type=MESH,
        )

    def copy3(e, d):
        return pltpu.make_async_remote_copy(
            src_ref=send3.at[peer(d)],
            dst_ref=recv3.at[e, d],
            send_sem=send3_sem.at[e, d],
            recv_sem=recv3_sem.at[e, d],
            device_id={"sta": peer(d), "tpl": fellow(e)},
            device_id_type=MESH,
        )

    loads[0].wait()
    build_hankel(wave_ref, record, hankel)
    loads[1].wait()
    correlate_blocks(blocks, stride, pattern_ref, hankel, corr)

    loads[2].wait()
    loads[3].wait()
    lane = lax.broadcasted_iota(jnp.int32, (count, LANES), 1)

    def shift(d):
        for k in range(groups):
            t = peer(d) * groups + k
            lag = lags_ref[t]
            begin = t * stride + (lag >> 7)
            rest = lag & (LANES - 1)
            near = corr[pl.ds(begin, count), :]
            after = corr[pl.ds(begin + 1, count), :]
            joined = pltpu.roll(jnp.where(lane >= rest, near, after), (LANES - rest) & (LANES - 1), 1)
            moved[d, k * count : (k + 1) * count, :] = joined * present_ref[t].astype(jnp.float32)

    far_first = sorted(range(1, n), key=lambda d: abs(d - n // 2))
    batch = max(n // 4, 1)
    for begin in range(0, n - 1, batch):
        for d in far_first[begin : begin + batch]:
            shift(d)
        if begin == 0:
            pl.semaphore_wait(barrier, n * m - 1)
        for d in far_first[begin : begin + batch]:
            copy1(d).start()
    shift(0)

    def gather1(d, acc):
        copy1(d).wait_recv()
        return acc + recv1[d]

    stack = lax.fori_loop(1, n, gather1, moved[0])
    scales = deviation_scale(stack, groups, n * own)
    scored[chunk:, :] = jnp.zeros((8, LANES), jnp.float32)
    for t in range(groups):
        scored[t * count : (t + 1) * count, :] = stack[t * count : (t + 1) * count, :] / scales[t]
    scale = jnp.concatenate(scales, axis=0)
    lane = lax.broadcasted_iota(jnp.int32, (groups, LANES), 1)
    for j in range(n):
        begin, rest = divmod(own * j, LANES)
        near = scored[pl.ds(begin, groups, stride=count), :]
        if rest:
            after = scored[pl.ds(begin + 1, groups, stride=count), :]
            near = pltpu.roll(jnp.where(lane >= rest, near, after), LANES - rest, 1)
        send2[j] = jnp.where(lane < own, near, scale)
        send3[j] = jnp.max(near, axis=0, keepdims=True)

    for e in range(1, m):

        def start3(d, carry):
            copy3(e, d).start()
            return carry

        lax.fori_loop(0, n, start3, 0)
    def start2(d, carry):
        copy2(d).start()
        return carry

    lax.fori_loop(1, n, start2, 0)
    recv2[me] = send2[me]

    def wait2(d, carry):
        copy2(d).wait_recv()
        return carry

    lax.fori_loop(1, n, wait2, 0)
    top = recv2[0]
    out_ref[:groups, :] = top
    for i in range(1, n):
        out_ref[i * groups : (i + 1) * groups, :] = recv2[i]
        top = jnp.maximum(top, recv2[i])
    top = jnp.max(top, axis=0, keepdims=True)
    for e in range(1, m):

        def wait3(d, best):
            copy3(e, d).wait_recv()
            return jnp.maximum(best, recv3[e, d])

        top = lax.fori_loop(0, n, wait3, top)
    lane = lax.broadcasted_iota(jnp.int32, (8, LANES), 1)
    moved_top = jnp.broadcast_to(pltpu.roll(top, LANES // 2, 1), (8, LANES))
    out_ref[:8, :] = jnp.where(lane < LANES // 2, out_ref[:8, :], moved_top)

    def finish(d, carry):
        copy1(d).wait_send()
        copy2(d).wait_send()
        return carry

    lax.fori_loop(1, n, finish, 0)
    for e in range(1, m):

        def finish3(d, carry):
            copy3(e, d).wait_send()
            return carry

        lax.fori_loop(0, n, finish3, 0)


def stack_and_score(wave, pattern, lags, present, n, m):
    chans, samples = wave.shape
    rows = pattern.shape[0]
    total = TOUT_DEV * n
    blocks = -(-(total + LAG) // (2 * LANES))
    span = 2 * LANES * blocks + LEN - LANES
    padded = span + LANES
    count = total // LANES
    stride = max(2 * blocks, LAG // LANES + count + 2) | 1
    groups = rows // n
    chunk = groups * count
    vmem = pl.BlockSpec(memory_space=pltpu.VMEM)
    return pl.pallas_call(
        functools.partial(stack_kernel, n, m, TOUT_DEV, blocks, stride),
        out_shape=jax.ShapeDtypeStruct((rows, LANES), jnp.float32),
        in_specs=[pl.BlockSpec(memory_space=pl.ANY)] * 4,
        out_specs=vmem,
        scratch_shapes=[
            pltpu.SMEM(lags.shape, lags.dtype),
            pltpu.SMEM(present.shape, present.dtype),
            pltpu.VMEM(wave.shape, wave.dtype),
            pltpu.VMEM(pattern.shape, pattern.dtype),
            pltpu.SemaphoreType.DMA((4,)),
            pltpu.VMEM((chans, padded), jnp.float32),
            pltpu.VMEM((chans, LANES, span), jnp.bfloat16),
            pltpu.VMEM((rows * stride, LANES), jnp.float32),
            pltpu.VMEM((n, chunk, LANES), jnp.float32),
            pltpu.VMEM((n, chunk, LANES), jnp.float32),
            pltpu.VMEM((chunk + 8, LANES), jnp.float32),
            pltpu.VMEM((n, groups, LANES), jnp.float32),
            pltpu.VMEM((n, groups, LANES), jnp.float32),
            pltpu.VMEM((n, 1, LANES), jnp.float32),
            pltpu.VMEM((m, n, 1, LANES), jnp.float32),
            pltpu.SemaphoreType.DMA((n,)),
            pltpu.SemaphoreType.DMA((n,)),
            pltpu.SemaphoreType.DMA((n,)),
            pltpu.SemaphoreType.DMA((n,)),
            pltpu.SemaphoreType.DMA((m, n)),
            pltpu.SemaphoreType.DMA((m, n)),
        ],
        compiler_params=pltpu.CompilerParams(collective_id=0, has_side_effects=True),
    )(lags, present, wave, pattern)


def finish_kernel(grid_ref, score_ref, scale_ref, peak_ref):
    own, rows = score_ref.shape
    turned = grid_ref[...].T
    score_ref[...] = turned[:own, :]
    scale_ref[...] = turned[own, :]
    peak_ref[...] = grid_ref[0, LANES // 2 : LANES // 2 + own]


def on_device(waveform, templates, lags, present):
    n, m = lax.axis_size("sta"), lax.axis_size("tpl")
    rows = templates.shape[0]
    grid = stack_and_score(waveform[0], templates[:, 0, :], lags[:, 0], present[:, 0], n, m)
    return pl.pallas_call(
        finish_kernel,
        out_shape=(
            jax.ShapeDtypeStruct((TOUT_DEV, rows), jnp.float32),
            jax.ShapeDtypeStruct((rows,), jnp.float32),
            jax.ShapeDtypeStruct((TOUT_DEV,), jnp.float32),
        ),
    )(grid)


def solution(mesh):
    placed = (P("sta", None, None), P("tpl", "sta", None), P("tpl", "sta"), P("tpl", "sta"))
    return jax.shard_map(
        on_device,
        mesh=mesh,
        in_specs=placed,
        out_specs=(P("sta", "tpl"), P("tpl"), P("sta")),
        check_vma=False,
    )
```

profile of v0, /device:TPU:0, one launch (start us, length us, event | category | flops | bytes accessed | tf_op | source)
XLA Modules:
  0.0 23.2 jit_solution(188294580288461309)
XLA Ops:
  0.6 21.1 %shard_map.67.grid_ref = f32[64,128]{1,0:T(8,128)} custom-call(s32[64]{0:T(128)} %bitcast.6, s32[64]{0:T(128)} %bitcast.7, bf16[3,4279]{1,0:T(4,128)(2,1)} %bitcast.5, bf16[64,1536]{1,0:T(8,128)(2,1)} %bitcast.4), custom_call_target="tpu_custom_call" | custom-call | tf_op jit(solution)/shard_map/pallas_call | solution.py:283
  21.7 1.5 %shard_map.68 = (f32[48,64]{1,0:T(8,128)}, f32[64]{0:T(128)}, f32[48]{0:T(128)}) custom-call(f32[64,128]{1,0:T(8,128)} %shard_map.67.grid_ref), custom_call_target="tpu_custom_call" | custom-call | tf_op jit(solution)/shard_map/pallas_call | solution.py:327
where the time goes:
time: 23.4 us; the launch traced here: 23.2 us
  Pallas kernels  22.6 us (97%)
  between operations  0.64 us (3%)
    pallas_call x1, Pallas kernels, stack_and_score(): pl.pallas_call(functools.partial(stack_kernel, n, m, TOUT_DEV, blocks, st...  21.1 us
    pallas_call x1, Pallas kernels, on_device(): pl.pallas_call(finish_kernel, out_shape=(jax.ShapeDtypeStruct((TOUT_DEV,...  1.47 us

commit v1 on v0

--- a/solution.py
+++ b/solution.py
@@ -21,24 +21,21 @@
 
 def build_hankel(wave_ref, record, hankel):
     chans, samples = wave_ref.shape
-    padded = record.shape[1]
     span = hankel.shape[2]
     record[...] = jnp.zeros_like(record)
     record[:, :samples] = wave_ref[...].astype(jnp.float32)
-    piece = span
-    for c in range(chans):
-        for start in range(0, span, piece):
-            size = min(piece, span - start)
-            wide = size + LANES
-            row = lax.broadcasted_iota(jnp.int32, (8, wide), 0)
+    piece = 8 * LANES
+    for start in range(0, span, piece):
+        size = min(piece, span - start)
+        wide = size + LANES
+        row = lax.broadcasted_iota(jnp.int32, (8, wide), 0)
+        for c in range(chans):
             base = jnp.broadcast_to(record[c : c + 1, start : start + wide], (8, wide))
             for bit in (1, 2, 4):
                 base = jnp.where((row & bit) != 0, pltpu.roll(base, wide - bit, 1), base)
+            both = jnp.concatenate([base, pltpu.roll(base, wide - 8, 1)], axis=0).astype(jnp.bfloat16)
             for g in range(LANES // 16):
-                low = pltpu.roll(base, wide - 16 * g, 1) if g else base
-                high = pltpu.roll(base, wide - 16 * g - 8, 1)
-                both = jnp.concatenate([low[:, :size], high[:, :size]], axis=0)
-                hankel[c, 16 * g : 16 * g + 16, start : start + size] = both.astype(jnp.bfloat16)
+                hankel[c, 16 * g : 16 * g + 16, start : start + size] = both[:, 16 * g : 16 * g + size]
 
 
 def correlate_blocks(blocks, stride, pattern_ref, hankel, corr):
@@ -47,16 +44,25 @@
     pattern = pattern_ref[...]
     wide = pattern.astype(jnp.float32)
     factor = 1.0 / jnp.sqrt(jnp.sum(wide * wide, axis=1, keepdims=True) + 1e-06)
-    for b in range(blocks):
+    depth = 2 * LANES
+    halves = []
+    for h in range(LEN // depth):
+        halves.append(jnp.concatenate([pattern[:, c * LEN + h * depth : c * LEN + (h + 1) * depth] for c in range(chans)], axis=1))
+    stacked = jnp.concatenate(halves, axis=0)
+    pending = None
+    for b in range(blocks + 1):
+        begin = depth * b
         parts = []
         for c in range(chans):
-            for q in range(LEN // LANES):
-                begin = 2 * LANES * b + LANES * q
-                parts.append(hankel[c, :, begin : begin + 2 * LANES])
+            for q in range(2):
+                parts.append(hankel[c, :, begin + LANES * q : begin + LANES * q + depth])
         columns = jnp.concatenate(parts, axis=0)
-        result = jnp.dot(pattern, columns, preferred_element_type=jnp.float32) * factor
-        corr[pl.ds(2 * b, rows, stride=stride), :] = result[:, :LANES]
-        corr[pl.ds(2 * b + 1, rows, stride=stride), :] = result[:, LANES:]
+        result = jnp.dot(stacked, columns, preferred_element_type=jnp.float32)
+        if b:
+            total = (pending + result[rows:]) * factor
+            corr[pl.ds(2 * b - 2, rows, stride=stride), :] = total[:, :LANES]
+            corr[pl.ds(2 * b - 1, rows, stride=stride), :] = total[:, LANES:]
+        pending = result[:rows]
 
 
 def deviation_scale(stack, groups, total):
@@ -105,15 +111,51 @@
     return scales
 
 
-def stack_kernel(n, m, own, blocks, stride, lags_hbm, present_hbm, wave_hbm, pattern_hbm, out_ref, lags_ref, present_ref, wave_ref, pattern_ref, load_sem, record, hankel, corr, moved, recv1, scored, send2, recv2, send3, recv3, send1_sem, recv1_sem, send2_sem, recv2_sem, send3_sem, recv3_sem):
+LEVELS = 32600.0
+ROUNDER = 12582912.0
+CODE_STEP = 64.0
+
+
+def encode(pieces, target, slot):
+    half = len(pieces) // 2
+    rows = pieces[0].shape[0]
+    most = jnp.abs(pieces[0])
+    for piece in pieces[1:]:
+        most = jnp.maximum(most, jnp.abs(piece))
+    most = jnp.maximum(jnp.max(most, axis=0, keepdims=True), 1e-30)
+    code = jnp.floor(jnp.log2(most) * CODE_STEP) + 1.0
+    inverse = LEVELS * jnp.exp2(code * (-1.0 / CODE_STEP))
+    for p in range(half):
+        high = (pieces[p] * inverse + ROUNDER).astype(jnp.int32)
+        low = (pieces[p + half] * inverse + ROUNDER).astype(jnp.int32)
+        target[slot, p * rows : (p + 1) * rows, :] = (high << 16) | (low & 65535)
+    target[slot, half * rows : half * rows + 1, :] = code.astype(jnp.int32)
+
+
+def decode(source, slot, half, rows):
+    code = source[slot, half * rows : half * rows + 1, :].astype(jnp.float32)
+    scale = jnp.exp2(code * (1.0 / CODE_STEP)) * (1.0 / LEVELS)
+    highs, lows = [], []
+    for p in range(half):
+        word = source[slot, p * rows : (p + 1) * rows, :]
+        highs.append((word >> 16).astype(jnp.float32) * scale)
+        lows.append(((word << 16) >> 16).astype(jnp.float32) * scale)
+    return highs + lows
+
+
+def stack_kernel(n, m, own, blocks, stride, lags_hbm, present_hbm, wave_hbm, pattern_hbm, out_ref, lags_ref, present_ref, wave_ref, pattern_ref, load_sem, record, hankel, corr, packed, recv1, scored, send2, recv2, send3, recv3, send_sem, recv1_sem, recv2_sem, recv3_sem):
     me, group = lax.axis_index("sta"), lax.axis_index("tpl")
     groups = send2.shape[1]
-    chunk = moved.shape[1]
-    count = chunk // groups
-    rows = n * groups
+    rows = pattern_ref.shape[0]
+    count = n * own // LANES
+    chunk = groups * count
+    pieces = max(groups, 2)
+    split = pieces // groups
+    piece_rows = chunk // pieces
+    half = pieces // 2
 
     def peer(d):
-        return lax.rem(me + d, n)
+        return me ^ d
 
     def fellow(e):
         return lax.rem(group + e, m)
@@ -136,13 +178,31 @@
 
         lax.fori_loop(0 if e else 1, n, greet, 0)
 
-    def copy1(d):
-        return pltpu.make_async_remote_copy(
-            src_ref=moved.at[d],
+    bands = []
+    low = 1
+    while low < n:
+        bands.append((low, min(2 * low, n)))
+        low *= 2
+    if len(bands) > 2:
+        bands[:2] = [(1, bands[1][1])]
+
+    def copy1(d, band):
+        return pltpu.make_async_remote_copy(
+            src_ref=packed.at[d],
             dst_ref=recv1.at[d],
-            send_sem=send1_sem.at[d],
-            recv_sem=recv1_sem.at[d],
+            send_sem=send_sem.at[0],
+            recv_sem=recv1_sem.at[band],
             device_id={"sta": peer(d), "tpl": group},
+            device_id_type=MESH,
+        )
+
+    def all1(low, high, band):
+        return pltpu.make_async_remote_copy(
+            src_ref=packed.at[pl.ds(low, high - low)],
+            dst_ref=recv1.at[pl.ds(low, high - low)],
+            send_sem=send_sem.at[0],
+            recv_sem=recv1_sem.at[band],
+            device_id={"sta": peer(1), "tpl": group},
             device_id_type=MESH,
         )
 
@@ -150,19 +210,39 @@
         return pltpu.make_async_remote_copy(
             src_ref=send2.at[peer(d)],
             dst_ref=recv2.at[me],
-            send_sem=send2_sem.at[d],
-            recv_sem=recv2_sem.at[d],
+            send_sem=send_sem.at[1],
+            recv_sem=recv2_sem,
             device_id={"sta": peer(d), "tpl": group},
             device_id_type=MESH,
         )
 
+    def all2():
+        return pltpu.make_async_remote_copy(
+            src_ref=send2.at[pl.ds(1, n - 1)],
+            dst_ref=recv2.at[pl.ds(1, n - 1)],
+            send_sem=send_sem.at[1],
+            recv_sem=recv2_sem,
+            device_id={"sta": peer(1), "tpl": group},
+            device_id_type=MESH,
+        )
+
     def copy3(e, d):
         return pltpu.make_async_remote_copy(
             src_ref=send3.at[peer(d)],
-            dst_ref=recv3.at[e, d],
-            send_sem=send3_sem.at[e, d],
-            recv_sem=recv3_sem.at[e, d],
+            dst_ref=recv3.at[e - 1, d],
+            send_sem=send_sem.at[2],
+            recv_sem=recv3_sem,
             device_id={"sta": peer(d), "tpl": fellow(e)},
+            device_id_type=MESH,
+        )
+
+    def all3():
+        return pltpu.make_async_remote_copy(
+            src_ref=recv3,
+            dst_ref=recv3,
+            send_sem=send_sem.at[2],
+            recv_sem=recv3_sem,
+            device_id={"sta": peer(1), "tpl": group},
             device_id_type=MESH,
         )
 
@@ -173,35 +253,37 @@
 
     loads[2].wait()
     loads[3].wait()
-    lane = lax.broadcasted_iota(jnp.int32, (count, LANES), 1)
-
-    def shift(d):
-        for k in range(groups):
-            t = peer(d) * groups + k
+    lane = lax.broadcasted_iota(jnp.int32, (piece_rows, LANES), 1)
+
+    def shifted(d):
+        found = []
+        for p in range(pieces):
+            t = peer(d) * groups + p // split
             lag = lags_ref[t]
-            begin = t * stride + (lag >> 7)
+            begin = t * stride + (lag >> 7) + (p % split) * piece_rows
             rest = lag & (LANES - 1)
-            near = corr[pl.ds(begin, count), :]
-            after = corr[pl.ds(begin + 1, count), :]
+            near = corr[pl.ds(begin, piece_rows), :]
+            after = corr[pl.ds(begin + 1, piece_rows), :]
             joined = pltpu.roll(jnp.where(lane >= rest, near, after), (LANES - rest) & (LANES - 1), 1)
-            moved[d, k * count : (k + 1) * count, :] = joined * present_ref[t].astype(jnp.float32)
-
-    far_first = sorted(range(1, n), key=lambda d: abs(d - n // 2))
+            found.append(joined * present_ref[t].astype(jnp.float32))
+        return found
+
     batch = max(n // 4, 1)
+    order = list(range(n - 1, 0, -1))
     for begin in range(0, n - 1, batch):
-        for d in far_first[begin : begin + batch]:
-            shift(d)
+        for d in order[begin : begin + batch]:
+            encode(shifted(d), packed, d)
         if begin == 0:
             pl.semaphore_wait(barrier, n * m - 1)
-        for d in far_first[begin : begin + batch]:
-            copy1(d).start()
-    shift(0)
-
-    def gather1(d, acc):
-        copy1(d).wait_recv()
-        return acc + recv1[d]
-
-    stack = lax.fori_loop(1, n, gather1, moved[0])
+        for d in order[begin : begin + batch]:
+            band = next(k for k, (a, b) in enumerate(bands) if a <= d < b)
+            copy1(d, band).start()
+    total = shifted(0)
+    for k, (low, high) in enumerate(bands):
+        all1(low, high, k).wait_recv()
+        for d in range(low, high):
+            total = [a + b for a, b in zip(total, decode(recv1, d, half, piece_rows))]
+    stack = jnp.concatenate(total, axis=0)
     scales = deviation_scale(stack, groups, n * own)
     scored[chunk:, :] = jnp.zeros((8, LANES), jnp.float32)
     for t in range(groups):
@@ -217,55 +299,40 @@
         send2[j] = jnp.where(lane < own, near, scale)
         send3[j] = jnp.max(near, axis=0, keepdims=True)
 
-    for e in range(1, m):
-
-        def start3(d, carry):
-            copy3(e, d).start()
-            return carry
-
-        lax.fori_loop(0, n, start3, 0)
-    def start2(d, carry):
+    if m == 2:
+        for d in range(n - 1, -1, -1):
+            copy3(1, d).start()
+    else:
+        for e in range(1, m):
+
+            def start3(d, carry):
+                copy3(e, d).start()
+                return carry
+
+            lax.fori_loop(0, n, start3, 0)
+    for d in range(n - 1, 0, -1):
         copy2(d).start()
-        return carry
-
-    lax.fori_loop(1, n, start2, 0)
     recv2[me] = send2[me]
-
-    def wait2(d, carry):
-        copy2(d).wait_recv()
-        return carry
-
-    lax.fori_loop(1, n, wait2, 0)
+    all1(1, n, 0).wait_send()
+
+    all2().wait_recv()
     top = recv2[0]
     out_ref[:groups, :] = top
     for i in range(1, n):
         out_ref[i * groups : (i + 1) * groups, :] = recv2[i]
         top = jnp.maximum(top, recv2[i])
     top = jnp.max(top, axis=0, keepdims=True)
-    for e in range(1, m):
-
-        def wait3(d, best):
-            copy3(e, d).wait_recv()
-            return jnp.maximum(best, recv3[e, d])
-
-        top = lax.fori_loop(0, n, wait3, top)
+    if m > 1:
+        all3().wait_recv()
+        for e in range(m - 1):
+            top = jnp.maximum(top, jnp.max(recv3[e], axis=0))
     lane = lax.broadcasted_iota(jnp.int32, (8, LANES), 1)
     moved_top = jnp.broadcast_to(pltpu.roll(top, LANES // 2, 1), (8, LANES))
     out_ref[:8, :] = jnp.where(lane < LANES // 2, out_ref[:8, :], moved_top)
 
-    def finish(d, carry):
-        copy1(d).wait_send()
-        copy2(d).wait_send()
-        return carry
-
-    lax.fori_loop(1, n, finish, 0)
-    for e in range(1, m):
-
-        def finish3(d, carry):
-            copy3(e, d).wait_send()
-            return carry
-
-        lax.fori_loop(0, n, finish3, 0)
+    all2().wait_send()
+    if m > 1:
+        all3().wait_send()
 
 
 def stack_and_score(wave, pattern, lags, present, n, m):
@@ -273,12 +340,13 @@
     rows = pattern.shape[0]
     total = TOUT_DEV * n
     blocks = -(-(total + LAG) // (2 * LANES))
-    span = 2 * LANES * blocks + LEN - LANES
-    padded = span + LANES
+    span = 2 * LANES * (blocks + 1) + LANES
+    padded = ceil_to(max(span + LANES, samples), LANES)
     count = total // LANES
     stride = max(2 * blocks, LAG // LANES + count + 2) | 1
     groups = rows // n
     chunk = groups * count
+    words = chunk // 2 + 1
     vmem = pl.BlockSpec(memory_space=pltpu.VMEM)
     return pl.pallas_call(
         functools.partial(stack_kernel, n, m, TOUT_DEV, blocks, stride),
@@ -294,19 +362,17 @@
             pltpu.VMEM((chans, padded), jnp.float32),
             pltpu.VMEM((chans, LANES, span), jnp.bfloat16),
             pltpu.VMEM((rows * stride, LANES), jnp.float32),
-            pltpu.VMEM((n, chunk, LANES), jnp.float32),
-            pltpu.VMEM((n, chunk, LANES), jnp.float32),
+            pltpu.VMEM((n, words, LANES), jnp.int32),
+            pltpu.VMEM((n, words, LANES), jnp.int32),
             pltpu.VMEM((chunk + 8, LANES), jnp.float32),
             pltpu.VMEM((n, groups, LANES), jnp.float32),
             pltpu.VMEM((n, groups, LANES), jnp.float32),
             pltpu.VMEM((n, 1, LANES), jnp.float32),
-            pltpu.VMEM((m, n, 1, LANES), jnp.float32),
-            pltpu.SemaphoreType.DMA((n,)),
-            pltpu.SemaphoreType.DMA((n,)),
-            pltpu.SemaphoreType.DMA((n,)),
-            pltpu.SemaphoreType.DMA((n,)),
-            pltpu.SemaphoreType.DMA((m, n)),
-            pltpu.SemaphoreType.DMA((m, n)),
+            pltpu.VMEM((max(m - 1, 1), n, 1, LANES), jnp.float32),
+            pltpu.SemaphoreType.DMA((3,)),
+            pltpu.SemaphoreType.DMA((max((n - 1).bit_length() - 1, 1),)),
+            pltpu.SemaphoreType.DMA,
+            pltpu.SemaphoreType.DMA,
         ],
         compiler_params=pltpu.CompilerParams(collective_id=0, has_side_effects=True),
     )(lags, present, wave, pattern)

time: 23.4 us -> 21.8 us (0.932)
  Pallas kernels: 22.6 us -> 21 us
    pallas_call x1, Pallas kernels: 21.1 us -> 19.5 us  [stack_and_score(): pl.pallas_call(functools.partial(stack_kernel, n, m, TOUT_DEV, blocks, st...]
where the time goes in v1:
time: 21.8 us; the launch traced here: 21.7 us
  Pallas kernels  21 us (96%)
  between operations  0.64 us (3%)
    pallas_call x1, Pallas kernels, stack_and_score(): pl.pallas_call(functools.partial(stack_kernel, n, m, TOUT_DEV, blocks, st...  19.5 us
    pallas_call x1, Pallas kernels, on_device(): pl.pallas_call(finish_kernel, out_shape=(jax.ShapeDtypeStruct((TOUT_DEV,...  1.47 us

profile of v1, /device:TPU:0, one launch (start us, length us, event | category | flops | bytes accessed | tf_op | source)
XLA Modules:
  0.0 21.7 jit_solution(14601742367961656482)
XLA Ops:
  0.6 19.5 %shard_map.67.grid_ref = f32[64,128]{1,0:T(8,128)} custom-call(s32[64]{0:T(128)} %bitcast.6, s32[64]{0:T(128)} %bitcast.7, bf16[3,4279]{1,0:T(4,128)(2,1)} %bitcast.5, bf16[64,1536]{1,0:T(8,128)(2,1)} %bitcast.4), custom_call_target="tpu_custom_call" | custom-call | tf_op jit(solution)/shard_map/pallas_call | solution.py:351
  20.2 1.5 %shard_map.68 = (f32[48,64]{1,0:T(8,128)}, f32[64]{0:T(128)}, f32[48]{0:T(128)}) custom-call(f32[64,128]{1,0:T(8,128)} %shard_map.67.grid_ref), custom_call_target="tpu_custom_call" | custom-call | tf_op jit(solution)/shard_map/pallas_call | solution.py:393

commit v2 on v1

--- a/solution.py
+++ b/solution.py
@@ -12,6 +12,7 @@
 BINS = 1024
 TOUT_DEV = 48
 LANES = 128
+VMEM_LIMIT = 16 * 1024 * 1024
 MESH = pl.DeviceIdType.MESH
 
 
@@ -19,50 +20,73 @@
     return -(-value // step) * step
 
 
-def build_hankel(wave_ref, record, hankel):
+def build_hankel(record, hankel, first, last):
+    back = lax.broadcasted_iota(jnp.int32, (8, LANES), 1) - lax.broadcasted_iota(jnp.int32, (8, LANES), 0)
+
+    def turned(c, j, a):
+        line = jnp.broadcast_to(record[c : c + 1, j * LANES : (j + 1) * LANES], (8, LANES))
+        return pltpu.roll(line, LANES - 7 - 8 * a, 1, stride=1, stride_axis=0)
+
+    for c in range(hankel.shape[0]):
+        for g in range(LANES // 16):
+            halves = []
+            for a in (2 * g, 2 * g + 1):
+                now = turned(c, first, a)
+                pieces = []
+                for j in range(first, last):
+                    later = turned(c, j + 1, a)
+                    pieces.append(jnp.where(back < LANES - 7 - 8 * a, now, later))
+                    now = later
+                halves.append(jnp.concatenate(pieces, axis=1))
+            hankel[c, 16 * g : 16 * g + 16, first * LANES : last * LANES] = jnp.concatenate(halves, axis=0).astype(jnp.bfloat16)
+
+
+def reverse_eights(pattern):
+    rows, width = pattern.shape
+    source = lax.broadcasted_iota(jnp.int32, (LANES, LANES), 0)
+    target = lax.broadcasted_iota(jnp.int32, (LANES, LANES), 1)
+    swap = (source == (target ^ 7)).astype(jnp.float32).astype(jnp.bfloat16)
+    chunks = jnp.concatenate([pattern[:, k * LANES : (k + 1) * LANES] for k in range(width // LANES)], axis=0)
+    turned = jnp.dot(chunks, swap, preferred_element_type=jnp.float32).astype(jnp.bfloat16)
+    return [turned[k * rows : (k + 1) * rows] for k in range(width // LANES)]
+
+
+def correlate(blocks, stride, wave_ref, pattern_ref, record, hankel, corr):
     chans, samples = wave_ref.shape
+    rows = pattern_ref.shape[0]
     span = hankel.shape[2]
     record[...] = jnp.zeros_like(record)
     record[:, :samples] = wave_ref[...].astype(jnp.float32)
-    piece = 8 * LANES
-    for start in range(0, span, piece):
-        size = min(piece, span - start)
-        wide = size + LANES
-        row = lax.broadcasted_iota(jnp.int32, (8, wide), 0)
-        for c in range(chans):
-            base = jnp.broadcast_to(record[c : c + 1, start : start + wide], (8, wide))
-            for bit in (1, 2, 4):
-                base = jnp.where((row & bit) != 0, pltpu.roll(base, wide - bit, 1), base)
-            both = jnp.concatenate([base, pltpu.roll(base, wide - 8, 1)], axis=0).astype(jnp.bfloat16)
-            for g in range(LANES // 16):
-                hankel[c, 16 * g : 16 * g + 16, start : start + size] = both[:, 16 * g : 16 * g + size]
-
-
-def correlate_blocks(blocks, stride, pattern_ref, hankel, corr):
-    chans = hankel.shape[0]
-    rows = pattern_ref.shape[0]
     pattern = pattern_ref[...]
     wide = pattern.astype(jnp.float32)
     factor = 1.0 / jnp.sqrt(jnp.sum(wide * wide, axis=1, keepdims=True) + 1e-06)
     depth = 2 * LANES
-    halves = []
-    for h in range(LEN // depth):
-        halves.append(jnp.concatenate([pattern[:, c * LEN + h * depth : c * LEN + (h + 1) * depth] for c in range(chans)], axis=1))
-    stacked = jnp.concatenate(halves, axis=0)
+    chunks = reverse_eights(pattern)
+    per = LEN // LANES
+    stacked = []
+    for c in range(chans):
+        halves = [jnp.concatenate([chunks[c * per + 2 * h + q] for q in range(2)], axis=1) for h in range(LEN // depth)]
+        stacked.append(jnp.concatenate(halves, axis=0))
+    built = 0
     pending = None
-    for b in range(blocks + 1):
-        begin = depth * b
-        parts = []
-        for c in range(chans):
-            for q in range(2):
-                parts.append(hankel[c, :, begin + LANES * q : begin + LANES * q + depth])
-        columns = jnp.concatenate(parts, axis=0)
-        result = jnp.dot(stacked, columns, preferred_element_type=jnp.float32)
-        if b:
-            total = (pending + result[rows:]) * factor
-            corr[pl.ds(2 * b - 2, rows, stride=stride), :] = total[:, :LANES]
-            corr[pl.ds(2 * b - 1, rows, stride=stride), :] = total[:, LANES:]
-        pending = result[:rows]
+    for first in range(0, blocks + 1, 2):
+        begin = depth * first
+        width = depth * min(2, blocks + 1 - first)
+        need = begin + width + LANES
+        build_hankel(record, hankel, built // LANES, need // LANES)
+        built = need
+        for b in range(first, first + width // depth):
+            piece = None
+            for c in range(chans):
+                start = depth * b
+                columns = jnp.concatenate([hankel[c, :, start + LANES * q : start + LANES * q + depth] for q in range(2)], axis=0)
+                part = jnp.dot(stacked[c], columns, preferred_element_type=jnp.float32)
+                piece = part if piece is None else piece + part
+            if b:
+                total = (pending + piece[rows:]) * factor
+                corr[pl.ds(2 * b - 2, rows, stride=stride), :] = total[:, :LANES]
+                corr[pl.ds(2 * b - 1, rows, stride=stride), :] = total[:, LANES:]
+            pending = piece[:rows]
 
 
 def deviation_scale(stack, groups, total):
@@ -170,13 +194,10 @@
         load.start()
 
     barrier = pltpu.get_barrier_semaphore()
-    for e in range(m):
-
-        def greet(d, carry):
-            pl.semaphore_signal(barrier, inc=1, device_id={"sta": peer(d), "tpl": fellow(e)}, device_id_type=MESH)
-            return carry
-
-        lax.fori_loop(0 if e else 1, n, greet, 0)
+    for d in range(n - 1, 0, -1):
+        pl.semaphore_signal(barrier, inc=1, device_id={"sta": peer(d), "tpl": group}, device_id_type=MESH)
+    for e in range(1, m):
+        pl.semaphore_signal(barrier, inc=1, device_id={"sta": me, "tpl": fellow(e)}, device_id_type=MESH)
 
     bands = []
     low = 1
@@ -247,9 +268,8 @@
         )
 
     loads[0].wait()
-    build_hankel(wave_ref, record, hankel)
     loads[1].wait()
-    correlate_blocks(blocks, stride, pattern_ref, hankel, corr)
+    correlate(blocks, stride, wave_ref, pattern_ref, record, hankel, corr)
 
     loads[2].wait()
     loads[3].wait()
@@ -274,7 +294,7 @@
         for d in order[begin : begin + batch]:
             encode(shifted(d), packed, d)
         if begin == 0:
-            pl.semaphore_wait(barrier, n * m - 1)
+            pl.semaphore_wait(barrier, n + m - 2)
         for d in order[begin : begin + batch]:
             band = next(k for k, (a, b) in enumerate(bands) if a <= d < b)
             copy1(d, band).start()
@@ -350,8 +370,8 @@
     vmem = pl.BlockSpec(memory_space=pltpu.VMEM)
     return pl.pallas_call(
         functools.partial(stack_kernel, n, m, TOUT_DEV, blocks, stride),
-        out_shape=jax.ShapeDtypeStruct((rows, LANES), jnp.float32),
-        in_specs=[pl.BlockSpec(memory_space=pl.ANY)] * 4,
+        out_shape=pltpu.VMEM((rows, LANES), jnp.float32),
+        in_specs=[pl.BlockSpec(memory_space=pltpu.HBM)] * 4,
         out_specs=vmem,
         scratch_shapes=[
             pltpu.SMEM(lags.shape, lags.dtype),
@@ -397,6 +417,8 @@
             jax.ShapeDtypeStruct((rows,), jnp.float32),
             jax.ShapeDtypeStruct((TOUT_DEV,), jnp.float32),
         ),
+        in_specs=[pl.BlockSpec(memory_space=pltpu.VMEM)],
+        compiler_params=pltpu.CompilerParams(vmem_limit_bytes=VMEM_LIMIT),
     )(grid)
 
 

time: 21.8 us -> 17.8 us (0.82)
  Pallas kernels: 21 us -> 17 us
    pallas_call x1, Pallas kernels: 19.5 us -> 16.3 us  [stack_and_score(): pl.pallas_call(functools.partial(stack_kernel, n, m, TOUT_DEV, blocks, st...]
    pallas_call x1, Pallas kernels: 1.47 us -> 0.71 us  [on_device(): pl.pallas_call(finish_kernel, out_shape=(jax.ShapeDtypeStruct((TOUT_DEV,...]
where the time goes in v2:
time: 17.8 us; the launch traced here: 17.6 us
  Pallas kernels  17 us (96%)
  between operations  0.64 us (4%)
    pallas_call x1, Pallas kernels, stack_and_score(): pl.pallas_call(functools.partial(stack_kernel, n, m, TOUT_DEV, blocks, st...  16.3 us
    pallas_call x1, Pallas kernels, on_device(): pl.pallas_call(finish_kernel, out_shape=(jax.ShapeDtypeStruct((TOUT_DEV,...  0.71 us

profile of v2, /device:TPU:0, one launch (start us, length us, event | category | flops | bytes accessed | tf_op | source)
XLA Modules:
  0.0 17.6 jit_solution(11614783292786892118)
XLA Ops:
  0.6 16.3 %shard_map.67.grid_ref = f32[64,128]{1,0:T(8,128)S(1)} custom-call(s32[64]{0:T(128)} %bitcast.6, s32[64]{0:T(128)} %bitcast.7, bf16[3,4279]{1,0:T(4,128)(2,1)} %bitcast.5, bf16[64,1536]{1,0:T(8,128)(2,1)} %bitcast.4), custom_call_target="tpu_custom_call" | custom-call | tf_op jit(solution)/shard_map/pallas_call | solution.py:371
  16.9 0.7 %shard_map.68 = (f32[48,64]{1,0:T(8,128)}, f32[64]{0:T(128)}, f32[48]{0:T(128)}) custom-call(f32[64,128]{1,0:T(8,128)S(1)} %shard_map.67.grid_ref), custom_call_target="tpu_custom_call" | custom-call | tf_op jit(solution)/shard_map/pallas_call | solution.py:413

commit v3 on v2

--- a/solution.py
+++ b/solution.py
@@ -21,7 +21,9 @@
 
 
 def build_hankel(record, hankel, first, last):
-    back = lax.broadcasted_iota(jnp.int32, (8, LANES), 1) - lax.broadcasted_iota(jnp.int32, (8, LANES), 0)
+    row = lax.broadcasted_iota(jnp.int32, (16, LANES), 0)
+    back = (lax.broadcasted_iota(jnp.int32, (16, LANES), 1) + row - 2 * (row & 7)).astype(jnp.float32).astype(jnp.bfloat16)
+    back = jnp.concatenate([back] * (last - first), axis=1)
 
     def turned(c, j, a):
         line = jnp.broadcast_to(record[c : c + 1, j * LANES : (j + 1) * LANES], (8, LANES))
@@ -29,16 +31,11 @@
 
     for c in range(hankel.shape[0]):
         for g in range(LANES // 16):
-            halves = []
-            for a in (2 * g, 2 * g + 1):
-                now = turned(c, first, a)
-                pieces = []
-                for j in range(first, last):
-                    later = turned(c, j + 1, a)
-                    pieces.append(jnp.where(back < LANES - 7 - 8 * a, now, later))
-                    now = later
-                halves.append(jnp.concatenate(pieces, axis=1))
-            hankel[c, 16 * g : 16 * g + 16, first * LANES : last * LANES] = jnp.concatenate(halves, axis=0).astype(jnp.bfloat16)
+            halves = [jnp.concatenate([turned(c, j, a) for j in range(first, last + 1)], axis=1) for a in (2 * g, 2 * g + 1)]
+            both = jnp.concatenate(halves, axis=0).astype(jnp.bfloat16)
+            hankel[c, 16 * g : 16 * g + 16, first * LANES : last * LANES] = jnp.where(
+                back < float(LANES - 7 - 16 * g), both[:, :-LANES], both[:, LANES:]
+            )
 
 
 def reverse_eights(pattern):
@@ -69,11 +66,18 @@
         stacked.append(jnp.concatenate(halves, axis=0))
     built = 0
     pending = None
-    for first in range(0, blocks + 1, 2):
-        begin = depth * first
-        width = depth * min(2, blocks + 1 - first)
-        need = begin + width + LANES
-        build_hankel(record, hankel, built // LANES, need // LANES)
+    starts = list(range(0, blocks + 1, 16))
+    pending = None
+
+    def upto(k):
+        last = min(starts[k] + 16, blocks + 1) if k < len(starts) else blocks + 1
+        return depth * last + LANES
+
+    for k, first in enumerate(starts):
+        width = depth * (min(first + 16, blocks + 1) - first)
+        need = upto(k + 0)
+        if need > built:
+            build_hankel(record, hankel, built // LANES, need // LANES)
         built = need
         for b in range(first, first + width // depth):
             piece = None
@@ -83,10 +87,13 @@
                 part = jnp.dot(stacked[c], columns, preferred_element_type=jnp.float32)
                 piece = part if piece is None else piece + part
             if b:
-                total = (pending + piece[rows:]) * factor
+                total = pending + piece[rows:] * factor
                 corr[pl.ds(2 * b - 2, rows, stride=stride), :] = total[:, :LANES]
                 corr[pl.ds(2 * b - 1, rows, stride=stride), :] = total[:, LANES:]
-            pending = piece[:rows]
+            pending = piece[:rows] * factor
+
+
+FINE = 16
 
 
 def deviation_scale(stack, groups, total):
@@ -94,44 +101,45 @@
     count = stack.shape[0] // groups
     position = jnp.clip(jnp.abs(stack) / width - 0.5, 0.0, BINS - 1.0)
     lower = jnp.minimum(jnp.floor(position), BINS - 2.0)
-    coarse = jnp.floor(lower * 0.125)
-    fine = position - 8.0 * coarse
-    sub = lax.broadcasted_iota(jnp.int32, (LANES, LANES), 0).astype(jnp.float32)
-    few = lax.broadcasted_iota(jnp.int32, (16, LANES), 0).astype(jnp.float32)
-    tables = []
-    for t in range(groups):
-        hots, weights = [], []
-        for a in range(count):
-            r = t * count + a
-            hots.append((coarse[r : r + 1, :] == sub).astype(jnp.float32).astype(jnp.bfloat16))
-            hat = jnp.maximum(1.0 - jnp.abs(fine[r : r + 1, :] - few), 0.0)
-            first = hat.astype(jnp.bfloat16)
-            left = hat - first.astype(jnp.float32)
-            second = left.astype(jnp.bfloat16)
-            third = (left - second.astype(jnp.float32)).astype(jnp.bfloat16)
-            weights.append(jnp.concatenate([first, second, third], axis=0))
-        hot = jnp.concatenate(hots, axis=1)
-        weight = jnp.concatenate(weights, axis=1)
-        found = lax.dot_general(weight, hot, (((1,), (1,)), ((), ())), preferred_element_type=jnp.float32)
-        found = found[:16] + found[16:32] + found[32:48]
-        tables.append(found[:8] + pltpu.roll(found[8:], 1, 1))
-    counts = jnp.concatenate(tables, axis=0)
-    row = lax.broadcasted_iota(jnp.int32, counts.shape, 0) & 7
-    running = counts
-    for step in (1, 2, 4):
-        running = running + jnp.where(row >= step, pltpu.roll(running, step, 0), 0.0)
-    sums = [jnp.broadcast_to(jnp.sum(t, axis=0, keepdims=True), (8, LANES)) for t in tables]
-    sums = jnp.concatenate(sums, axis=0)
-    upper = (
-        lax.broadcasted_iota(jnp.int32, (LANES, LANES), 0) < lax.broadcasted_iota(jnp.int32, (LANES, LANES), 1)
-    ).astype(jnp.float32)
-    prior = jnp.dot(sums, upper, precision=lax.Precision.HIGHEST, preferred_element_type=jnp.float32)
-    earlier = prior + (running - counts)
-    share = jnp.clip((0.5 * total - earlier) / jnp.maximum(counts, 1.0), 0.0, 1.0)
+    share = position - lower
+    head = share.astype(jnp.bfloat16).astype(jnp.float32)
+    tail = share - head
+    coarse = jnp.floor(lower * (1.0 / FINE))
+    fine = lower - FINE * coarse
+    broad = lax.broadcasted_iota(jnp.int32, (BINS // FINE, LANES), 0).astype(jnp.float32)
+    few = lax.broadcasted_iota(jnp.int32, (FINE, LANES), 0).astype(jnp.float32)
+    row = lax.broadcasted_iota(jnp.int32, (FINE, LANES), 0)
+    lane = lax.broadcasted_iota(jnp.int32, (FINE, LANES), 1)
     scales = []
     for t in range(groups):
-        part = jnp.sum(share[8 * t : 8 * t + 8], axis=0, keepdims=True)
-        scales.append(1.4826 * (width * jnp.sum(part, axis=1, keepdims=True)))
+        below, weights = [], []
+        for r in range(t * count, (t + 1) * count):
+            below.append((coarse[r : r + 1, :] <= broad).astype(jnp.float32).astype(jnp.bfloat16))
+            upto = (fine[r : r + 1, :] <= few).astype(jnp.float32)
+            same = fine[r : r + 1, :] == few
+            parts = [upto, same.astype(jnp.float32), jnp.where(same, head[r : r + 1, :], 0.0), jnp.where(same, tail[r : r + 1, :], 0.0)]
+            weights.append(jnp.concatenate(parts, axis=0).astype(jnp.bfloat16))
+        weight = jnp.concatenate(weights, axis=1)
+        below = jnp.concatenate(below, axis=1)
+        found = lax.dot_general(weight, below, (((1,), (1,)), ((), ())), preferred_element_type=jnp.float32)
+        if found.shape[1] < LANES:
+            found = jnp.concatenate([found, jnp.zeros((found.shape[0], LANES - found.shape[1]), jnp.float32)], axis=1)
+        upto, same = found[:FINE], found[FINE : 2 * FINE]
+        part = found[2 * FINE : 3 * FINE] + found[3 * FINE :]
+        upto_left = jnp.where(lane >= 1, pltpu.roll(upto, 1, 1), 0.0)
+        same_left = jnp.where(lane >= 1, pltpu.roll(same, 1, 1), 0.0)
+        part_left = jnp.where(lane >= 1, pltpu.roll(part, 1, 1), 0.0)
+        part_far = jnp.where(lane >= 2, pltpu.roll(part, 2, 1), 0.0)
+        held = same - same_left
+        moved = part - part_left
+        spilled = pltpu.roll(jnp.where(row == FINE - 1, part_left - part_far, moved), 1, 0)
+        counts = held - moved + spilled
+        prior = upto_left[FINE - 1 : FINE, :]
+        earlier = prior + (upto - upto_left) - held - spilled
+        portion = jnp.clip((0.5 * total - earlier) / jnp.maximum(counts, 1.0), 0.0, 1.0)
+        portion = jnp.where(lane < BINS // FINE, portion, 0.0)
+        portion = jnp.sum(portion, axis=0, keepdims=True)
+        scales.append(1.4826 * (width * jnp.sum(portion, axis=1, keepdims=True)))
     return scales
 
 
@@ -303,19 +311,23 @@
         all1(low, high, k).wait_recv()
         for d in range(low, high):
             total = [a + b for a, b in zip(total, decode(recv1, d, half, piece_rows))]
-    stack = jnp.concatenate(total, axis=0)
-    scales = deviation_scale(stack, groups, n * own)
+    for p in range(pieces):
+        scored[p * piece_rows : (p + 1) * piece_rows, :] = total[p]
     scored[chunk:, :] = jnp.zeros((8, LANES), jnp.float32)
-    for t in range(groups):
-        scored[t * count : (t + 1) * count, :] = stack[t * count : (t + 1) * count, :] / scales[t]
-    scale = jnp.concatenate(scales, axis=0)
+    stack = scored[:chunk, :]
     lane = lax.broadcasted_iota(jnp.int32, (groups, LANES), 1)
+    views = []
     for j in range(n):
         begin, rest = divmod(own * j, LANES)
         near = scored[pl.ds(begin, groups, stride=count), :]
         if rest:
             after = scored[pl.ds(begin + 1, groups, stride=count), :]
             near = pltpu.roll(jnp.where(lane >= rest, near, after), LANES - rest, 1)
+        views.append(near)
+    scale = jnp.concatenate(deviation_scale(stack, groups, n * own), axis=0)
+    inverse = 1.0 / scale
+    for j in range(n):
+        near = views[j] * inverse
         send2[j] = jnp.where(lane < own, near, scale)
         send3[j] = jnp.max(near, axis=0, keepdims=True)
 

time: 17.8 us -> 17.4 us (0.978)
  Pallas kernels: 17 us -> 16.6 us
    pallas_call x1, Pallas kernels: 16.3 us -> 15.9 us  [stack_and_score(): pl.pallas_call(functools.partial(stack_kernel, n, m, TOUT_DEV, blocks, st...]
where the time goes in v3:
time: 17.4 us; the launch traced here: 17.2 us
  Pallas kernels  16.6 us (95%)
  between operations  0.64 us (4%)
    pallas_call x1, Pallas kernels, stack_and_score(): pl.pallas_call(functools.partial(stack_kernel, n, m, TOUT_DEV, blocks, st...  15.9 us
    pallas_call x1, Pallas kernels, on_device(): pl.pallas_call(finish_kernel, out_shape=(jax.ShapeDtypeStruct((TOUT_DEV,...  0.71 us

profile of v3, /device:TPU:0, one launch (start us, length us, event | category | flops | bytes accessed | tf_op | source)
XLA Modules:
  0.0 17.2 jit_solution(4661023513786816892)
XLA Ops:
  0.6 15.9 %shard_map.67.grid_ref = f32[64,128]{1,0:T(8,128)S(1)} custom-call(s32[64]{0:T(128)} %bitcast.6, s32[64]{0:T(128)} %bitcast.7, bf16[3,4279]{1,0:T(4,128)(2,1)} %bitcast.5, bf16[64,1536]{1,0:T(8,128)(2,1)} %bitcast.4), custom_call_target="tpu_custom_call" | custom-call | tf_op jit(solution)/shard_map/pallas_call | solution.py:383
  16.5 0.7 %shard_map.68 = (f32[48,64]{1,0:T(8,128)}, f32[64]{0:T(128)}, f32[48]{0:T(128)}) custom-call(f32[64,128]{1,0:T(8,128)S(1)} %shard_map.67.grid_ref), custom_call_target="tpu_custom_call" | custom-call | tf_op jit(solution)/shard_map/pallas_call | solution.py:425

commit v4 on v3

--- a/solution.py
+++ b/solution.py
@@ -48,34 +48,35 @@
     return [turned[k * rows : (k + 1) * rows] for k in range(width // LANES)]
 
 
-def correlate(blocks, stride, wave_ref, pattern_ref, record, hankel, corr):
+def correlate(blocks, stride, wave_ref, pattern_ref, record, hankel, corr, load):
     chans, samples = wave_ref.shape
     rows = pattern_ref.shape[0]
     span = hankel.shape[2]
     record[...] = jnp.zeros_like(record)
     record[:, :samples] = wave_ref[...].astype(jnp.float32)
+    depth = 2 * LANES
+    built = depth * min(4, blocks + 1) + LANES
+    build_hankel(record, hankel, 0, built // LANES)
+    load.wait()
     pattern = pattern_ref[...]
     wide = pattern.astype(jnp.float32)
     factor = 1.0 / jnp.sqrt(jnp.sum(wide * wide, axis=1, keepdims=True) + 1e-06)
-    depth = 2 * LANES
     chunks = reverse_eights(pattern)
     per = LEN // LANES
     stacked = []
     for c in range(chans):
         halves = [jnp.concatenate([chunks[c * per + 2 * h + q] for q in range(2)], axis=1) for h in range(LEN // depth)]
         stacked.append(jnp.concatenate(halves, axis=0))
-    built = 0
+    starts = list(range(0, blocks + 1, 2))
     pending = None
-    starts = list(range(0, blocks + 1, 16))
-    pending = None
 
     def upto(k):
-        last = min(starts[k] + 16, blocks + 1) if k < len(starts) else blocks + 1
+        last = min(starts[k] + 2, blocks + 1) if k < len(starts) else blocks + 1
         return depth * last + LANES
 
     for k, first in enumerate(starts):
-        width = depth * (min(first + 16, blocks + 1) - first)
-        need = upto(k + 0)
+        width = depth * (min(first + 2, blocks + 1) - first)
+        need = upto(k + 1)
         if need > built:
             build_hankel(record, hankel, built // LANES, need // LANES)
         built = need
@@ -151,40 +152,48 @@
 def encode(pieces, target, slot):
     half = len(pieces) // 2
     rows = pieces[0].shape[0]
-    most = jnp.abs(pieces[0])
-    for piece in pieces[1:]:
-        most = jnp.maximum(most, jnp.abs(piece))
-    most = jnp.maximum(jnp.max(most, axis=0, keepdims=True), 1e-30)
-    code = jnp.floor(jnp.log2(most) * CODE_STEP) + 1.0
-    inverse = LEVELS * jnp.exp2(code * (-1.0 / CODE_STEP))
+    codes, inverses = [], []
+    for group in (pieces[:half], pieces[half:]):
+        most = jnp.abs(group[0])
+        for piece in group[1:]:
+            most = jnp.maximum(most, jnp.abs(piece))
+        most = jnp.maximum(jnp.max(most, axis=0, keepdims=True), 1e-30)
+        code = jnp.floor(jnp.log2(most) * CODE_STEP) + 1.0
+        inverses.append(LEVELS * jnp.exp2(code * (-1.0 / CODE_STEP)))
+        codes.append(code.astype(jnp.int32))
     for p in range(half):
-        high = (pieces[p] * inverse + ROUNDER).astype(jnp.int32)
-        low = (pieces[p + half] * inverse + ROUNDER).astype(jnp.int32)
+        high = (pieces[p] * inverses[0] + ROUNDER).astype(jnp.int32)
+        low = (pieces[p + half] * inverses[1] + ROUNDER).astype(jnp.int32)
         target[slot, p * rows : (p + 1) * rows, :] = (high << 16) | (low & 65535)
-    target[slot, half * rows : half * rows + 1, :] = code.astype(jnp.int32)
+    target[slot, half * rows : half * rows + 1, :] = (codes[0] << 16) | (codes[1] & 65535)
 
 
 def decode(source, slot, half, rows):
-    code = source[slot, half * rows : half * rows + 1, :].astype(jnp.float32)
-    scale = jnp.exp2(code * (1.0 / CODE_STEP)) * (1.0 / LEVELS)
+    def split(word):
+        return (word >> 16).astype(jnp.float32), ((word << 16) >> 16).astype(jnp.float32)
+
+    scales = [jnp.exp2(code * (1.0 / CODE_STEP)) * (1.0 / LEVELS) for code in split(source[slot, half * rows : half * rows + 1, :])]
     highs, lows = [], []
     for p in range(half):
-        word = source[slot, p * rows : (p + 1) * rows, :]
-        highs.append((word >> 16).astype(jnp.float32) * scale)
-        lows.append(((word << 16) >> 16).astype(jnp.float32) * scale)
+        high, low = split(source[slot, p * rows : (p + 1) * rows, :])
+        highs.append(high * scales[0])
+        lows.append(low * scales[1])
     return highs + lows
 
 
 def stack_kernel(n, m, own, blocks, stride, lags_hbm, present_hbm, wave_hbm, pattern_hbm, out_ref, lags_ref, present_ref, wave_ref, pattern_ref, load_sem, record, hankel, corr, packed, recv1, scored, send2, recv2, send3, recv3, send_sem, recv1_sem, recv2_sem, recv3_sem):
     me, group = lax.axis_index("sta"), lax.axis_index("tpl")
-    groups = send2.shape[1]
+    owners = n // 2
+    quarter = n // 4
+    half = send2.shape[1]
+    groups = 2 * half
     rows = pattern_ref.shape[0]
     count = n * own // LANES
     chunk = groups * count
-    pieces = max(groups, 2)
-    split = pieces // groups
-    piece_rows = chunk // pieces
-    half = pieces // 2
+    upper = (me >= owners).astype(jnp.int32)
+    virtual = upper * quarter + lax.rem(me, quarter)
+    owner = jnp.logical_and(me >= quarter, me < 3 * quarter)
+    outer = 1 - owner.astype(jnp.int32)
 
     def peer(d):
         return me ^ d
@@ -202,169 +211,177 @@
         load.start()
 
     barrier = pltpu.get_barrier_semaphore()
-    for d in range(n - 1, 0, -1):
-        pl.semaphore_signal(barrier, inc=1, device_id={"sta": peer(d), "tpl": group}, device_id_type=MESH)
+
+    @pl.when(owner)
+    def greet():
+        for d in range(n - 1, 0, -1):
+            pl.semaphore_signal(barrier, inc=1, device_id={"sta": peer(d), "tpl": group}, device_id_type=MESH)
+
     for e in range(1, m):
         pl.semaphore_signal(barrier, inc=1, device_id={"sta": me, "tpl": fellow(e)}, device_id_type=MESH)
 
-    bands = []
-    low = 1
-    while low < n:
-        bands.append((low, min(2 * low, n)))
-        low *= 2
-    if len(bands) > 2:
-        bands[:2] = [(1, bands[1][1])]
-
-    def copy1(d, band):
+    def move(source, target, send, recv, sta, tpl):
         return pltpu.make_async_remote_copy(
-            src_ref=packed.at[d],
-            dst_ref=recv1.at[d],
-            send_sem=send_sem.at[0],
-            recv_sem=recv1_sem.at[band],
-            device_id={"sta": peer(d), "tpl": group},
+            src_ref=source,
+            dst_ref=target,
+            send_sem=send_sem.at[send],
+            recv_sem=recv,
+            device_id={"sta": sta, "tpl": tpl},
             device_id_type=MESH,
         )
 
-    def all1(low, high, band):
-        return pltpu.make_async_remote_copy(
-            src_ref=packed.at[pl.ds(low, high - low)],
-            dst_ref=recv1.at[pl.ds(low, high - low)],
-            send_sem=send_sem.at[0],
-            recv_sem=recv1_sem.at[band],
-            device_id={"sta": peer(1), "tpl": group},
-            device_id_type=MESH,
-        )
-
-    def copy2(d):
-        return pltpu.make_async_remote_copy(
-            src_ref=send2.at[peer(d)],
-            dst_ref=recv2.at[me],
-            send_sem=send_sem.at[1],
-            recv_sem=recv2_sem,
-            device_id={"sta": peer(d), "tpl": group},
-            device_id_type=MESH,
-        )
-
-    def all2():
-        return pltpu.make_async_remote_copy(
-            src_ref=send2.at[pl.ds(1, n - 1)],
-            dst_ref=recv2.at[pl.ds(1, n - 1)],
-            send_sem=send_sem.at[1],
-            recv_sem=recv2_sem,
-            device_id={"sta": peer(1), "tpl": group},
-            device_id_type=MESH,
-        )
-
-    def copy3(e, d):
-        return pltpu.make_async_remote_copy(
-            src_ref=send3.at[peer(d)],
-            dst_ref=recv3.at[e - 1, d],
-            send_sem=send_sem.at[2],
-            recv_sem=recv3_sem,
-            device_id={"sta": peer(d), "tpl": fellow(e)},
-            device_id_type=MESH,
-        )
-
-    def all3():
-        return pltpu.make_async_remote_copy(
-            src_ref=recv3,
-            dst_ref=recv3,
-            send_sem=send_sem.at[2],
-            recv_sem=recv3_sem,
-            device_id={"sta": peer(1), "tpl": group},
-            device_id_type=MESH,
-        )
+    def copy1(k):
+        band = 2 * outer + (1 if k >= quarter else 0)
+        return move(packed.at[k], recv1.at[outer * owners + k], 0, recv1_sem.at[band], quarter + (virtual ^ k), group)
+
+    def span1(low, high, band):
+        part = recv1.at[pl.ds(low, high - low)]
+        return move(part, part, 0, recv1_sem.at[band], peer(1), group)
+
+    def copy2(p):
+        return move(send2.at[p], recv2.at[virtual], 1, recv2_sem, p, group)
+
+    def span2(size):
+        part = recv2.at[pl.ds(0, size)]
+        return move(part, part, 1, recv2_sem, peer(1), group)
+
+    def copy3(e, p):
+        return move(send3.at[p], recv3.at[e - 1, virtual], 2, recv3_sem, p, fellow(e))
 
     loads[0].wait()
-    loads[1].wait()
-    correlate(blocks, stride, wave_ref, pattern_ref, record, hankel, corr)
+    correlate(blocks, stride, wave_ref, pattern_ref, record, hankel, corr, loads[1])
 
     loads[2].wait()
     loads[3].wait()
-    lane = lax.broadcasted_iota(jnp.int32, (piece_rows, LANES), 1)
-
-    def shifted(d):
+    lane = lax.broadcasted_iota(jnp.int32, (count, LANES), 1)
+
+    def shifted(k):
         found = []
-        for p in range(pieces):
-            t = peer(d) * groups + p // split
+        for p in range(groups):
+            t = (p // half) * (rows // 2) + (virtual ^ k) * half + p % half
             lag = lags_ref[t]
-            begin = t * stride + (lag >> 7) + (p % split) * piece_rows
+            begin = t * stride + (lag >> 7)
             rest = lag & (LANES - 1)
-            near = corr[pl.ds(begin, piece_rows), :]
-            after = corr[pl.ds(begin + 1, piece_rows), :]
+            near = corr[pl.ds(begin, count), :]
+            after = corr[pl.ds(begin + 1, count), :]
             joined = pltpu.roll(jnp.where(lane >= rest, near, after), (LANES - rest) & (LANES - 1), 1)
             found.append(joined * present_ref[t].astype(jnp.float32))
         return found
 
-    batch = max(n // 4, 1)
-    order = list(range(n - 1, 0, -1))
-    for begin in range(0, n - 1, batch):
-        for d in order[begin : begin + batch]:
-            encode(shifted(d), packed, d)
-        if begin == 0:
-            pl.semaphore_wait(barrier, n + m - 2)
-        for d in order[begin : begin + batch]:
-            band = next(k for k, (a, b) in enumerate(bands) if a <= d < b)
-            copy1(d, band).start()
-    total = shifted(0)
-    for k, (low, high) in enumerate(bands):
-        all1(low, high, k).wait_recv()
-        for d in range(low, high):
-            total = [a + b for a, b in zip(total, decode(recv1, d, half, piece_rows))]
-    for p in range(pieces):
-        scored[p * piece_rows : (p + 1) * piece_rows, :] = total[p]
-    scored[chunk:, :] = jnp.zeros((8, LANES), jnp.float32)
-    stack = scored[:chunk, :]
-    lane = lax.broadcasted_iota(jnp.int32, (groups, LANES), 1)
-    views = []
-    for j in range(n):
-        begin, rest = divmod(own * j, LANES)
-        near = scored[pl.ds(begin, groups, stride=count), :]
-        if rest:
-            after = scored[pl.ds(begin + 1, groups, stride=count), :]
-            near = pltpu.roll(jnp.where(lane >= rest, near, after), LANES - rest, 1)
-        views.append(near)
-    scale = jnp.concatenate(deviation_scale(stack, groups, n * own), axis=0)
-    inverse = 1.0 / scale
-    for j in range(n):
-        near = views[j] * inverse
-        send2[j] = jnp.where(lane < own, near, scale)
-        send3[j] = jnp.max(near, axis=0, keepdims=True)
-
-    if m == 2:
-        for d in range(n - 1, -1, -1):
-            copy3(1, d).start()
-    else:
-        for e in range(1, m):
-
-            def start3(d, carry):
-                copy3(e, d).start()
-                return carry
-
-            lax.fori_loop(0, n, start3, 0)
-    for d in range(n - 1, 0, -1):
-        copy2(d).start()
-    recv2[me] = send2[me]
-    all1(1, n, 0).wait_send()
-
-    all2().wait_recv()
+    order = sorted(range(1, owners), key=lambda k: (-(k & (quarter // 2)), -k))
+    encode(shifted(order[0]), packed, order[0])
+    pl.semaphore_wait(barrier, owners + m - 2 + outer)
+    copy1(order[0]).start()
+    begin, size = 1, 3
+    while begin < len(order):
+        batch = order[begin : begin + size]
+        for k in batch:
+            encode(shifted(k), packed, k)
+        for k in batch:
+            copy1(k).start()
+        begin += size
+
+    @pl.when(jnp.logical_not(owner))
+    def last():
+        encode(shifted(0), packed, 0)
+        copy1(0).start()
+
+    @pl.when(owner)
+    def serve():
+        total = shifted(0)
+        for band, low, high in ((0, 1, quarter), (1, quarter, owners), (2, owners, owners + quarter), (3, owners + quarter, n)):
+            span1(low, high, band).wait_recv()
+            for slot in range(low, high):
+                total = [a + b for a, b in zip(total, decode(recv1, slot, half, count))]
+        for p in range(groups):
+            scored[p * count : (p + 1) * count, :] = total[p]
+        scored[chunk:, :] = jnp.zeros((8, LANES), jnp.float32)
+        stack = scored[:chunk, :]
+        lane = lax.broadcasted_iota(jnp.int32, (half, LANES), 1)
+        middle = LANES // 2
+        views = []
+        for j in range(n):
+            begin, rest = divmod(own * j, LANES)
+            sides = []
+            for side in range(2):
+                first = side * half * count + begin
+                near = scored[pl.ds(first, half, stride=count), :]
+                if rest:
+                    after = scored[pl.ds(first + 1, half, stride=count), :]
+                    near = jnp.where(lane >= rest, near, after)
+                turn = (side * middle - rest) % LANES
+                sides.append(pltpu.roll(near, turn, 1) if turn else near)
+            views.append(jnp.where(lane < middle, sides[0], sides[1]))
+        scales = deviation_scale(stack, groups, n * own)
+        scale = jnp.where(lane < middle, jnp.concatenate(scales[:half], axis=0), jnp.concatenate(scales[half:], axis=0))
+        inverse = 1.0 / scale
+
+        def ready(targets):
+            for j in targets:
+                near = views[j] * inverse
+                send2[j] = jnp.where((lane & (middle - 1)) < own, near, scale)
+                send3[j] = jnp.max(near, axis=0, keepdims=True)
+
+        def leave(targets):
+            for p in targets:
+                if m == 2:
+                    copy3(1, p).start()
+                if quarter <= p < 3 * quarter:
+
+                    @pl.when(me != p)
+                    def start2():
+                        copy2(p).start()
+
+                else:
+                    copy2(p).start()
+
+        ready(range(quarter))
+        leave(range(quarter))
+        ready(range(quarter, n))
+        leave(range(quarter, n))
+        if m > 2:
+            for e in range(1, m):
+
+                def start3(p, carry):
+                    copy3(e, p).start()
+                    return carry
+
+                lax.fori_loop(0, n, start3, 0)
+        recv2[virtual] = send2[me]
+
+    @pl.when(owner)
+    def arrive_owner():
+        span2(owners - 1).wait_recv()
+
+    @pl.when(jnp.logical_not(owner))
+    def arrive():
+        span2(owners).wait_recv()
+
     top = recv2[0]
-    out_ref[:groups, :] = top
-    for i in range(1, n):
-        out_ref[i * groups : (i + 1) * groups, :] = recv2[i]
-        top = jnp.maximum(top, recv2[i])
+    for i in range(owners):
+        piece = recv2[i]
+        out_ref[i * half : (i + 1) * half, :] = piece
+        top = jnp.maximum(top, piece)
+    out_ref[rows // 2 :, :] = pltpu.roll(out_ref[: rows // 2, :], LANES // 2, 1)
     top = jnp.max(top, axis=0, keepdims=True)
     if m > 1:
-        all3().wait_recv()
+        move(recv3, recv3, 2, recv3_sem, peer(1), group).wait_recv()
         for e in range(m - 1):
             top = jnp.maximum(top, jnp.max(recv3[e], axis=0))
+    top = jnp.broadcast_to(jnp.maximum(top, pltpu.roll(top, LANES // 2, 1)), (8, LANES))
     lane = lax.broadcasted_iota(jnp.int32, (8, LANES), 1)
-    moved_top = jnp.broadcast_to(pltpu.roll(top, LANES // 2, 1), (8, LANES))
-    out_ref[:8, :] = jnp.where(lane < LANES // 2, out_ref[:8, :], moved_top)
-
-    all2().wait_send()
-    if m > 1:
-        all3().wait_send()
+    out_ref[:8, :] = jnp.where(lane < LANES // 2, out_ref[:8, :], top)
+
+    @pl.when(jnp.logical_not(owner))
+    def drain():
+        span1(0, owners, 0).wait_send()
+
+    @pl.when(owner)
+    def drain_owner():
+        span1(1, owners, 0).wait_send()
+        move(send2.at[pl.ds(0, n - 1)], send2.at[pl.ds(0, n - 1)], 1, recv2_sem, peer(1), group).wait_send()
+        for e in range(1, m):
+            move(send3, send3, 2, recv3_sem, peer(1), group).wait_send()
 
 
 def stack_and_score(wave, pattern, lags, present, n, m):
@@ -376,7 +393,8 @@
     padded = ceil_to(max(span + LANES, samples), LANES)
     count = total // LANES
     stride = max(2 * blocks, LAG // LANES + count + 2) | 1
-    groups = rows // n
+    owners = n // 2
+    groups = rows // owners
     chunk = groups * count
     words = chunk // 2 + 1
     vmem = pl.BlockSpec(memory_space=pltpu.VMEM)
@@ -394,15 +412,15 @@
             pltpu.VMEM((chans, padded), jnp.float32),
             pltpu.VMEM((chans, LANES, span), jnp.bfloat16),
             pltpu.VMEM((rows * stride, LANES), jnp.float32),
-            pltpu.VMEM((n, words, LANES), jnp.int32),
+            pltpu.VMEM((owners, words, LANES), jnp.int32),
             pltpu.VMEM((n, words, LANES), jnp.int32),
             pltpu.VMEM((chunk + 8, LANES), jnp.float32),
-            pltpu.VMEM((n, groups, LANES), jnp.float32),
-            pltpu.VMEM((n, groups, LANES), jnp.float32),
+            pltpu.VMEM((n, groups // 2, LANES), jnp.float32),
+            pltpu.VMEM((owners, groups // 2, LANES), jnp.float32),
             pltpu.VMEM((n, 1, LANES), jnp.float32),
-            pltpu.VMEM((max(m - 1, 1), n, 1, LANES), jnp.float32),
+            pltpu.VMEM((max(m - 1, 1), owners, 1, LANES), jnp.float32),
             pltpu.SemaphoreType.DMA((3,)),
-            pltpu.SemaphoreType.DMA((max((n - 1).bit_length() - 1, 1),)),
+            pltpu.SemaphoreType.DMA((4,)),
             pltpu.SemaphoreType.DMA,
             pltpu.SemaphoreType.DMA,
         ],

time: 17.4 us -> 16.8 us (0.966)
  Pallas kernels: 16.6 us -> 16 us
    pallas_call x1, Pallas kernels: 15.9 us -> 15.3 us  [stack_and_score(): pl.pallas_call(functools.partial(stack_kernel, n, m, TOUT_DEV, blocks, st...]
where the time goes in v4:
time: 16.8 us; the launch traced here: 16.7 us
  Pallas kernels  16 us (95%)
  between operations  0.64 us (4%)
    pallas_call x1, Pallas kernels, stack_and_score(): pl.pallas_call(functools.partial(stack_kernel, n, m, TOUT_DEV, blocks, st...  15.3 us
    pallas_call x1, Pallas kernels, on_device(): pl.pallas_call(finish_kernel, out_shape=(jax.ShapeDtypeStruct((TOUT_DEV,...  0.71 us

profile of v4, /device:TPU:0, one launch (start us, length us, event | category | flops | bytes accessed | tf_op | source)
XLA Modules:
  0.0 16.7 jit_solution(7579610748355068794)
XLA Ops:
  0.6 15.3 %shard_map.67.grid_ref = f32[64,128]{1,0:T(8,128)S(1)} custom-call(s32[64]{0:T(128)} %bitcast.6, s32[64]{0:T(128)} %bitcast.7, bf16[3,4279]{1,0:T(4,128)(2,1)} %bitcast.5, bf16[64,1536]{1,0:T(8,128)(2,1)} %bitcast.4), custom_call_target="tpu_custom_call" | custom-call | tf_op jit(solution)/shard_map/pallas_call | solution.py:401
  16.0 0.7 %shard_map.68 = (f32[48,64]{1,0:T(8,128)}, f32[64]{0:T(128)}, f32[48]{0:T(128)}) custom-call(f32[64,128]{1,0:T(8,128)S(1)} %shard_map.67.grid_ref), custom_call_target="tpu_custom_call" | custom-call | tf_op jit(solution)/shard_map/pallas_call | solution.py:443

commit v5 on v4

--- a/solution.py
+++ b/solution.py
@@ -181,7 +181,7 @@
     return highs + lows
 
 
-def stack_kernel(n, m, own, blocks, stride, lags_hbm, present_hbm, wave_hbm, pattern_hbm, out_ref, lags_ref, present_ref, wave_ref, pattern_ref, load_sem, record, hankel, corr, packed, recv1, scored, send2, recv2, send3, recv3, send_sem, recv1_sem, recv2_sem, recv3_sem):
+def stack_kernel(n, m, own, blocks, stride, lags_hbm, present_hbm, wave_hbm, pattern_hbm, score_ref, scale_ref, peak_ref, out_ref, lags_ref, present_ref, wave_ref, pattern_ref, load_sem, record, hankel, corr, packed, recv1, scored, send2, recv2, send3, recv3, send_sem, recv1_sem, recv2_sem, recv3_sem):
     me, group = lax.axis_index("sta"), lax.axis_index("tpl")
     owners = n // 2
     quarter = n // 4
@@ -364,13 +364,15 @@
         top = jnp.maximum(top, piece)
     out_ref[rows // 2 :, :] = pltpu.roll(out_ref[: rows // 2, :], LANES // 2, 1)
     top = jnp.max(top, axis=0, keepdims=True)
+    turned = out_ref[...].T
+    score_ref[...] = turned[:own, :]
+    scale_ref[...] = turned[own, :]
     if m > 1:
         move(recv3, recv3, 2, recv3_sem, peer(1), group).wait_recv()
         for e in range(m - 1):
             top = jnp.maximum(top, jnp.max(recv3[e], axis=0))
-    top = jnp.broadcast_to(jnp.maximum(top, pltpu.roll(top, LANES // 2, 1)), (8, LANES))
-    lane = lax.broadcasted_iota(jnp.int32, (8, LANES), 1)
-    out_ref[:8, :] = jnp.where(lane < LANES // 2, out_ref[:8, :], top)
+    top = jnp.maximum(top, pltpu.roll(top, LANES // 2, 1))
+    peak_ref[...] = top[0, :own]
 
     @pl.when(jnp.logical_not(owner))
     def drain():
@@ -400,10 +402,11 @@
     vmem = pl.BlockSpec(memory_space=pltpu.VMEM)
     return pl.pallas_call(
         functools.partial(stack_kernel, n, m, TOUT_DEV, blocks, stride),
-        out_shape=pltpu.VMEM((rows, LANES), jnp.float32),
+        out_shape=(pltpu.VMEM((TOUT_DEV, rows), jnp.float32), pltpu.VMEM((rows,), jnp.float32), pltpu.VMEM((TOUT_DEV,), jnp.float32)),
         in_specs=[pl.BlockSpec(memory_space=pltpu.HBM)] * 4,
-        out_specs=vmem,
+        out_specs=(vmem, vmem, vmem),
         scratch_shapes=[
+            pltpu.VMEM((rows, LANES), jnp.float32),
             pltpu.SMEM(lags.shape, lags.dtype),
             pltpu.SMEM(present.shape, present.dtype),
             pltpu.VMEM(wave.shape, wave.dtype),
@@ -428,28 +431,26 @@
     )(lags, present, wave, pattern)
 
 
-def finish_kernel(grid_ref, score_ref, scale_ref, peak_ref):
-    own, rows = score_ref.shape
-    turned = grid_ref[...].T
-    score_ref[...] = turned[:own, :]
-    scale_ref[...] = turned[own, :]
-    peak_ref[...] = grid_ref[0, LANES // 2 : LANES // 2 + own]
+def finish_kernel(score, scale, peak, score_out, scale_out, peak_out, sems):
+    pairs = ((score, score_out), (scale, scale_out), (peak, peak_out))
+    copies = [pltpu.make_async_copy(source, target, sems.at[k]) for k, (source, target) in enumerate(pairs)]
+    for copy in copies:
+        copy.start()
+    for copy in copies:
+        copy.wait()
 
 
 def on_device(waveform, templates, lags, present):
     n, m = lax.axis_size("sta"), lax.axis_size("tpl")
-    rows = templates.shape[0]
-    grid = stack_and_score(waveform[0], templates[:, 0, :], lags[:, 0], present[:, 0], n, m)
+    found = stack_and_score(waveform[0], templates[:, 0, :], lags[:, 0], present[:, 0], n, m)
     return pl.pallas_call(
         finish_kernel,
-        out_shape=(
-            jax.ShapeDtypeStruct((TOUT_DEV, rows), jnp.float32),
-            jax.ShapeDtypeStruct((rows,), jnp.float32),
-            jax.ShapeDtypeStruct((TOUT_DEV,), jnp.float32),
-        ),
-        in_specs=[pl.BlockSpec(memory_space=pltpu.VMEM)],
+        out_shape=tuple(jax.ShapeDtypeStruct(part.shape, part.dtype) for part in found),
+        in_specs=[pl.BlockSpec(memory_space=pltpu.VMEM)] * 3,
+        out_specs=(pl.BlockSpec(memory_space=pltpu.HBM),) * 3,
+        scratch_shapes=[pltpu.SemaphoreType.DMA((3,))],
         compiler_params=pltpu.CompilerParams(vmem_limit_bytes=VMEM_LIMIT),
-    )(grid)
+    )(*found)
 
 
 def solution(mesh):

time: 16.8 us -> 16.8 us (level)
  no operation moved by 1% of the time
where the time goes in v5:
time: 16.8 us; the launch traced here: 16.6 us
  Pallas kernels  16 us (95%)
  between operations  0.64 us (4%)
    pallas_call x1, Pallas kernels, stack_and_score(): pl.pallas_call(functools.partial(stack_kernel, n, m, TOUT_DEV, blocks, st...  15.3 us
    pallas_call x1, Pallas kernels, on_device(): pl.pallas_call(finish_kernel, out_shape=tuple((jax.ShapeDtypeStruct(part....  0.64 us

profile of v5, /device:TPU:0, one launch (start us, length us, event | category | flops | bytes accessed | tf_op | source)
XLA Modules:
  0.0 16.6 jit_solution(3933562454034601068)
XLA Ops:
  0.6 15.3 %shard_map.67 = (f32[48,64]{1,0:T(8,128)S(1)}, f32[64]{0:T(128)S(1)}, f32[48]{0:T(128)S(1)}) custom-call(s32[64]{0:T(128)} %bitcast.6, s32[64]{0:T(128)} %bitcast.7, bf16[3,4279]{1,0:T(4,128)(2,1)} %bitcast.5, bf16[64,1536]{1,0:T(8,128)(2,1)} %bitcast.4), custom_call_target="tpu_custom_call" | custom-call | tf_op jit(solution)/shard_map/pallas_call | solution.py:403
  16.0 0.6 %shard_map.68 = (f32[48,64]{1,0:T(8,128)}, f32[64]{0:T(128)}, f32[48]{0:T(128)}) custom-call(f32[48,64]{1,0:T(8,128)S(1)} %get-tuple-element.6.score, f32[64]{0:T(128)S(1)} %get-tuple-element.7.scale, f32[48]{0:T(128)S(1)} %get-tuple-element.8.peak), custom_call_target="tpu_custom_call" | custom-call | tf_op jit(solution)/shard_map/pallas_call | solution.py:446
